TPU v7x, 32 devices: a whole 2x2x4 slice. The times are simulated.
32 devices in a mesh: clip: 2 (over y), tm: 4 (over z), space: 2 (over x), chan: 2 (over core).
Axes of the slice: x: 2, y: 2, z: 4, core: 2. Of those that a mesh axis runs over, the one named last changes fastest.
Arguments:
- features: bfloat16 [16, 8, 90, 256], P(('clip', 'tm'), 'space'), parts along dimension 0, may hold values from -700 to 700
- hidden: bfloat16 [16, 8, 90, 256], P(('clip', 'tm'), 'space'), parts along dimension 0, may hold values from -700 to 700
- cotangent: bfloat16 [16, 8, 90, 256], P(('clip', 'tm'), 'space'), parts along dimension 0, may hold values from -6 to 6
- kernel_one: bfloat16 [256, 3, 3, 3, 256], P(None, None, None, None, 'chan'), may hold values from -0.078125 to 0.078125
- kernel_two: bfloat16 [256, 3, 3, 3, 256], P(None, None, None, None, 'chan'), may hold values from -0.078125 to 0.078125
- gains: float32 [2, 256], replicated, may hold values from 0.25 to 1.75
Outputs:
- feature_grad: bfloat16 [16, 8, 90, 256], P(('clip', 'tm'), 'space', None, 'chan'), parts along dimension 0
- delta_one: float32 [512, 3, 3, 3, 256], P(('clip', 'tm', 'space'), None, None, None, 'chan'), parts along dimension 0
- delta_two: float32 [512, 3, 3, 3, 256], P(('clip', 'tm', 'space'), None, None, None, 'chan'), parts along dimension 0
- gain_grads: float32 [4, 256], P('clip', 'chan'), parts along dimension 0
There are 2 independent parts, one for each index of `clip`. A program takes and returns all parts, laid end to end along the dimension named above; an argument that names none is the same for every part. Nothing has to cross between parts.
All inputs are finite; a program needn't handle non-finite values.
Results may differ from a plain program's by a relative error of at most 0.005.
Values may be sent and summed in bfloat16 or wider, within the bound.
A program may use at most 128 MiB of HBM per device.

v0:
```python
import jax
import jax.numpy as jnp
from jax import lax
from jax.sharding import PartitionSpec as P

GROUPS = 32


epsilon = 1e-06


def extended_2(cells, sides, width):
    for axis, dim in sides:
        count = lax.axis_size(axis)
        ends = count - 1
        head = lax.slice_in_dim(cells, 0, width, axis=dim)
        tail = lax.slice_in_dim(cells, cells.shape[dim] - width, cells.shape[dim], axis=dim)
        cells = jnp.concatenate(
            [
                lax.ppermute(tail, axis, [(i, (i + 1) % count) for i in range(ends)]),
                cells,
                lax.ppermute(head, axis, [((i + 1) % count, i) for i in range(ends)]),
            ],
            axis=dim,
        )
    return cells


def passed_along(block, axis, distance):
    devices = range(lax.axis_size(axis))
    route = [(i - distance, i) for i in devices if i - distance in devices]
    return lax.ppermute(block, axis, route)


def clip_totals(values):
    return lax.psum(values, ("tm", "space"))


def statistics(total, square, members, per):
    mean = jnp.sum(total.reshape(-1, per), axis=1) / members
    spread = jnp.sum(square.reshape(-1, per), axis=1) / members - mean * mean
    scale = lax.rsqrt(spread + epsilon)
    return (jnp.repeat(mean, per), jnp.repeat(scale, per))


def norm_back(upstream, centred, scaled, gain, scale, members, per):
    gate = jax.nn.sigmoid(scaled)
    slope = upstream * gate * (1.0 + scaled * (1.0 - gate))
    totals = clip_totals(
        jnp.stack([jnp.sum(slope, axis=(0, 1, 2)), jnp.sum(slope * centred, axis=(0, 1, 2))])
    )
    first = jnp.repeat(jnp.sum((gain * totals[0]).reshape(-1, per), axis=1), per) / members
    second = jnp.repeat(jnp.sum((gain * totals[1]).reshape(-1, per), axis=1), per) / members
    return (scale * (slope * gain - first - centred * second), totals[1])


def extend(grad):
    edged = extended_2(grad, (("space", 1),), 1)
    later = passed_along(edged, "tm", -1)
    joined = jnp.concatenate([edged, later], axis=0)
    return jnp.pad(joined, ((0, 0), (0, 0), (1, 1), (0, 0)))


def tap_stack(extended, frames, height, width):
    pieces = []
    for frame_tap in range(3):
        for row_tap in range(3):
            for col_tap in range(3):
                pieces.append(
                    extended[
                        2 - frame_tap : 2 - frame_tap + frames,
                        2 - row_tap : 2 - row_tap + height,
                        2 - col_tap : 2 - col_tap + width,
                    ]
                )
    stacked = jnp.stack(pieces, axis=3)
    return stacked.reshape(frames * height * width, 27, extended.shape[3])


def kernel_term(flat_active, taps):
    depth = taps.shape[2]
    flat_taps = taps.reshape(taps.shape[0], 27 * depth)

    def term(start, count):
        product = lax.dot_general(
            flat_active, flat_taps, (((0,), (0,)), ((), ())), preferred_element_type=jnp.float32
        )
        return product.reshape(count, 3, 3, 3, depth)

    return term


def layer_back(active, upstream, kernel, half):
    frames, height, width, channels = active.shape
    taps = tap_stack(extend(upstream), frames, height, width)
    flat_active = active.reshape(frames * height * width, channels)
    term = kernel_term(flat_active, taps)
    partial_grad = lax.dot_general(
        taps,
        kernel.reshape(channels, 27, half),
        (((1, 2), (1, 2)), ((), ())),
        preferred_element_type=jnp.float32,
    )
    back = lax.psum_scatter(
        partial_grad.reshape(frames, height, width, channels),
        "chan",
        scatter_dimension=3,
        tiled=True,
    )
    return (term, back)


def shards(features, hidden, cotangent, kernel_one, kernel_two, gains):
    frames, height, width, channels = features.shape
    half = kernel_one.shape[4]
    per = channels // GROUPS
    offset = lax.axis_index("chan") * half
    members = float(frames * height * width * per * lax.axis_size("tm") * lax.axis_size("space"))
    share = channels // (lax.axis_size("tm") * lax.axis_size("space"))

    def own(field):
        return lax.dynamic_slice_in_dim(field, offset, half, field.ndim - 1)

    field_one = features.astype(jnp.float32)
    field_two = hidden.astype(jnp.float32)
    totals = clip_totals(
        jnp.stack(
            [
                jnp.sum(field_one, axis=(0, 1, 2)),
                jnp.sum(field_one * field_one, axis=(0, 1, 2)),
                jnp.sum(field_two, axis=(0, 1, 2)),
                jnp.sum(field_two * field_two, axis=(0, 1, 2)),
            ]
        )
    )
    mean_one, scale_one = statistics(totals[0], totals[1], members, per)
    mean_two, scale_two = statistics(totals[2], totals[3], members, per)
    centred_one = (field_one - mean_one) * scale_one
    scaled_one = centred_one * gains[0]
    active_one = (scaled_one * jax.nn.sigmoid(scaled_one)).astype(jnp.bfloat16)
    centred_two = (field_two - mean_two) * scale_two
    scaled_two = centred_two * gains[1]
    active_two = (scaled_two * jax.nn.sigmoid(scaled_two)).astype(jnp.bfloat16)
    upstream_two = own(cotangent)
    term_two, back_two = layer_back(active_two, upstream_two, kernel_two, half)
    grad_two, weighted_two = norm_back(
        back_two, own(centred_two), own(scaled_two), own(gains[1]), own(scale_two), members, per
    )
    grad_hidden = grad_two.astype(jnp.bfloat16)
    term_one, back_one = layer_back(active_one, grad_hidden, kernel_one, half)
    start = jnp.int32(0)
    combined = lax.psum_scatter(
        jnp.stack(
            [
                term_one(start, lax.axis_size(("tm", "space")) * share),
                term_two(start, lax.axis_size(("tm", "space")) * share),
            ],
            axis=1,
        ),
        ("tm", "space"),
        scatter_dimension=0,
        tiled=True,
    )
    delta_one = combined[:, 0]
    delta_two = combined[:, 1]
    grad_one, weighted_one = norm_back(
        back_one, own(centred_one), own(scaled_one), own(gains[0]), own(scale_one), members, per
    )
    feature_grad = (own(cotangent).astype(jnp.float32) + grad_one).astype(jnp.bfloat16)
    return (feature_grad, delta_one, delta_two, jnp.stack([weighted_one, weighted_two]))


def solution(mesh):
    placed = (
        P(("clip", "tm"), "space", None, None),
        P(("clip", "tm"), "space", None, None),
        P(("clip", "tm"), "space", None, None),
        P(None, None, None, None, "chan"),
        P(None, None, None, None, "chan"),
        P(),
    )
    return jax.shard_map(
        shards,
        mesh=mesh,
        in_specs=placed,
        out_specs=(
            P(("clip", "tm"), "space", None, "chan"),
            P(("clip", "tm", "space"), None, None, None, "chan"),
            P(("clip", "tm", "space"), None, None, None, "chan"),
            P("clip", "chan"),
        ),
        check_vma=False,
    )
```

profile of v0, /device:TPU:0, one launch (start us, length us, event | category | flops | bytes accessed | tf_op | source)
XLA Modules:
  0.0 289.6 jit_solution(4879320679843734137)
XLA Ops:
  8.4 4.9 %collective-permute-start = (bf16[2,1,90,128]{3,2,1,0:T(8,128)(2,1)S(1)}, bf16[2,1,90,128]{3,2,1,0:T(8,128)(2,1)S(1)}, u32[]{:S(2)}, u32[]{:S(2)}) collective-permute-start(bf16[2,1,90,128]{3,2,1,0:T(8,128)(2,1)S(1)} %get-tuple-element.41), channel_id=1, source_target_pairs={{0,2},{1,3},{4,6},{5,7},{8,10},{9,11},{12,14},{13,15},{16,18},{17,... | collective-permute-start | bytes 138248 | tf_op jit(solution)/shard_map/ppermute | solution.py:20
  15.1 4.2 %collective-permute-done.1 = bf16[2,1,90,128]{3,2,1,0:T(8,128)(2,1)S(1)} collective-permute-done((bf16[2,1,90,128]{3,2,1,0:T(8,128)(2,1)S(1)}, bf16[2,1,90,128]{3,2,1,0:T(8,128)(2,1)S(1)}, u32[]{:S(2)}, u32[]{:S(2)}) %collective-permute-start.1) | collective-permute-done | bytes 46112 | tf_op jit(solution)/shard_map/ppermute | solution.py:22
  20.6 7.9 %collective-permute-done.2 = bf16[2,6,90,128]{3,2,1,0:T(8,128)(2,1)S(1)} collective-permute-done((bf16[2,6,90,128]{3,2,1,0:T(8,128)(2,1)S(1)}, bf16[2,6,90,128]{3,2,1,0:T(8,128)(2,1)S(1)}, u32[]{:S(2)}, u32[]{:S(2)}) %collective-permute-start.2) | collective-permute-done | bytes 276512 | tf_op jit(solution)/shard_map/ppermute | solution.py:32
  30.3 2.3 copy-done.3
  32.7 2.5 convolution_bitcast_fusion.2
  35.6 18.1 %psum.21 = f32[4,256]{1,0:T(4,128)S(1)} all-reduce(f32[4,256]{1,0:T(4,128)S(1)} %pad_maximum_fusion.8), channel_id=1, replica_groups=mesh['clip'=2,'tm'=4,'space'=2,'chan'=2] {'tm','space'}, use_global_device_ids=true, to_apply=%region_4.0 | all-reduce | flops 1024 | bytes 8192 | tf_op jit(solution)/shard_map/psum | solution.py:36
  56.8 18.2 %psum.22 = f32[2,128]{1,0:T(2,128)S(1)} all-reduce(f32[2,128]{1,0:T(2,128)S(1)} %pad_maximum_fusion.9), channel_id=1, replica_groups=mesh['clip'=2,'tm'=4,'space'=2,'chan'=2] {'tm','space'}, use_global_device_ids=true, to_apply=%region_12.13 | all-reduce | flops 256 | bytes 2048 | tf_op jit(solution)/shard_map/psum | solution.py:36
  75.9 2.9 collective-permute-start.3
  80.5 4.3 %collective-permute-done.4 = bf16[2,1,90,128]{3,2,1,0:T(8,128)(2,1)S(1)} collective-permute-done((bf16[2,1,90,128]{3,2,1,0:T(8,128)(2,1)S(1)}, bf16[2,1,90,128]{3,2,1,0:T(8,128)(2,1)S(1)}, u32[]{:S(2)}, u32[]{:S(2)}) %collective-permute-start.4) | collective-permute-done | bytes 46112 | tf_op jit(solution)/shard_map/ppermute | solution.py:22
  86.9 6.5 %collective-permute-done.5 = bf16[2,6,90,128]{3,2,1,0:T(8,128)(2,1)S(1)} collective-permute-done((bf16[2,6,90,128]{3,2,1,0:T(8,128)(2,1)S(1)}, bf16[2,6,90,128]{3,2,1,0:T(8,128)(2,1)S(1)}, u32[]{:S(2)}, u32[]{:S(2)}) %collective-permute-start.5) | collective-permute-done | bytes 276512 | tf_op jit(solution)/shard_map/ppermute | solution.py:32
  95.6 1.6 fusion
  99.3 4.6 %copy.72 = bf16[2,4,90,27,128]{4,3,2,1,0:T(8,128)(2,1)S(1)} copy(bf16[2,4,90,27,128]{4,2,3,1,0:T(8,128)(2,1)} %copy-done.3) | data formatting | bytes 9953280 | tf_op jit(solution)/shard_map/stack | solution.py:76
  103.9 7.3 %copy.111 = bf16[90,8,27,128]{3,1,2,0:T(8,128)(2,1)} copy(bf16[90,8,27,128]{3,2,1,0:T(8,128)(2,1)S(1)} %bitcast.258) | data formatting | bytes 9953280
  111.2 7.9 %copy.73 = bf16[3456,720]{1,0:T(8,128)(2,1)} copy(bf16[3456,720]{0,1:T(8,128)(2,1)} %bitcast.262) | data formatting | bytes 9953280 | tf_op jit(solution)/shard_map/dot_general | solution.py:85
  119.1 6.0 %convolution_bitcast_fusion = f32[256,1,3,3,3,128]{5,0,4,3,2,1:T(8,128)} fusion(bf16[3,3,3,128,720]{4,3,2,1,0:T(8,128)(2,1)} %bitcast.260, bf16[720,256,1,1,1]{1,0,2,3,4:T(8,128)(2,1)S(1)} %reshape.335), kind=kOutput, calls=%fused_computation.5 | convolution fusion | flops 1274019840 | bytes 8884224 | tf_op jit(solution)/shard_map/dot_general | solution.py:85
  125.1 5.8 %copy.69 = bf16[2,4,90,27,128]{4,3,2,1,0:T(8,128)(2,1)S(1)} copy(bf16[2,4,90,27,128]{4,2,1,0,3:T(8,128)(2,1)} %copy-done.4) | data formatting | bytes 9953280 | tf_op jit(solution)/shard_map/stack | solution.py:76
  130.9 7.3 %copy.112 = bf16[90,8,27,128]{3,1,2,0:T(8,128)(2,1)} copy(bf16[90,8,27,128]{3,2,1,0:T(8,128)(2,1)S(1)} %bitcast.259) | data formatting | bytes 9953280
  138.2 8.0 %copy.70 = bf16[3456,720]{1,0:T(8,128)(2,1)} copy(bf16[3456,720]{0,1:T(8,128)(2,1)} %bitcast.263) | data formatting | bytes 9953280 | tf_op jit(solution)/shard_map/dot_general | solution.py:85
  146.2 4.3 %convolution_bitcast_fusion.1 = f32[256,1,3,3,3,128]{5,0,4,3,2,1:T(8,128)S(1)} fusion(bf16[3,3,3,128,720]{4,3,2,1,0:T(8,128)(2,1)} %bitcast.261, bf16[720,256,1,1,1]{1,0,2,3,4:T(8,128)(2,1)S(1)} %reshape.334), kind=kOutput, calls=%fused_computation.6 | convolution fusion | flops 1274019840 | bytes 8884224 | tf_op jit(solution)/shard_map/dot_general | solution.py:85
  150.5 3.4 %pad_maximum_fusion = f32[256,2,3,3,3,128]{5,0,4,3,2,1:T(8,128)} fusion(f32[256,1,3,3,3,128]{5,0,4,3,2,1:T(8,128)S(1)} %copy-done.2, f32[256,1,3,3,3,128]{5,0,4,3,2,1:T(8,128)S(1)} %convolution_bitcast_fusion.1), kind=kLoop, calls=%fused_computation | loop fusion | flops 1769472 | bytes 14155776 | tf_op jit(solution)/shard_map/stack | solution.py:153
  154.0 2.0 fusion.36
  156.0 18.2 %psum.23 = f32[2,128]{1,0:T(2,128)S(1)} all-reduce(f32[2,128]{1,0:T(2,128)S(1)} %pad_maximum_fusion.10), channel_id=1, replica_groups=mesh['clip'=2,'tm'=4,'space'=2,'chan'=2] {'tm','space'}, use_global_device_ids=true, to_apply=%region_18.19 | all-reduce | flops 256 | bytes 2048 | tf_op jit(solution)/shard_map/psum | solution.py:36
  177.5 103.5 %reduce-scatter.8.cloned.1.call-done = f32[32,2,3,3,3,128]{5,0,4,3,2,1:T(8,128)} async-done(((f32[256,2,3,3,3,128]{5,0,4,3,2,1:T(8,128)}), f32[32,2,3,3,3,128]{5,0,4,3,2,1:T(8,128)}) %reduce-scatter.8.cloned.1.call-update) | async-done | bytes 884752 | tf_op jit(solution)/shard_map/reduce_scatter | solution.py:152
  281.0 2.1 slice_bitcast_fusion
  (158 shorter events, 21.5 us)
Async XLA Ops:
  7.2 23.1 %copy-start = (bf16[256,3,3,3,128]{4,0,3,2,1:T(8,128)(2,1)S(1)}, bf16[256,3,3,3,128]{4,0,3,2,1:T(8,128)(2,1)}, u32[]{:S(2)}) copy-start(bf16[256,3,3,3,128]{4,0,3,2,1:T(8,128)(2,1)} %param.10) | copy-start | bytes 5308420
  7.2 48.4 %reduce-scatter.4.cloned.1.call-start = ((), (), s32[]{:S(2)}) async-start(), calls=%async_computation.3 | async-start | bytes 1179648 | tf_op jit(solution)/shard_map/reduce_scatter | solution.py:104
  8.4 6.6 %collective-permute-start = (bf16[2,1,90,128]{3,2,1,0:T(8,128)(2,1)S(1)}, bf16[2,1,90,128]{3,2,1,0:T(8,128)(2,1)S(1)}, u32[]{:S(2)}, u32[]{:S(2)}) collective-permute-start(bf16[2,1,90,128]{3,2,1,0:T(8,128)(2,1)S(1)} %get-tuple-element.41), channel_id=1, source_target_pairs={{0,2},{1,3},{4,6},{5,7},{8,10},{9,11},{12,14},{13,15},{16,18},{17,... | collective-permute-start | bytes 138248 | tf_op jit(solution)/shard_map/ppermute | solution.py:20
  13.3 6.0 %collective-permute-start.1 = (bf16[2,1,90,128]{3,2,1,0:T(8,128)(2,1)S(1)}, bf16[2,1,90,128]{3,2,1,0:T(8,128)(2,1)S(1)}, u32[]{:S(2)}, u32[]{:S(2)}) collective-permute-start(bf16[2,1,90,128]{3,2,1,0:T(8,128)(2,1)S(1)} %get-tuple-element.40), channel_id=1, source_target_pairs={{2,0},{3,1},{6,4},{7,5},{10,8},{11,9},{14,12},{15,13},{18,16},{19,... | collective-permute-start | bytes 138248 | tf_op jit(solution)/shard_map/ppermute | solution.py:22
  19.3 9.2 %collective-permute-start.2 = (bf16[2,6,90,128]{3,2,1,0:T(8,128)(2,1)S(1)}, bf16[2,6,90,128]{3,2,1,0:T(8,128)(2,1)S(1)}, u32[]{:S(2)}, u32[]{:S(2)}) collective-permute-start(bf16[2,6,90,128]{3,2,1,0:T(8,128)(2,1)S(1)} %constant_dynamic-update-slice_fusion), channel_id=1, source_target_pairs={{4,0},{8,4},{12,8},{5,1},{9,5},{13,9},{6,2},{10,6},{14,10},{7,3},{... | collective-permute-start | bytes 829448 | tf_op jit(solution)/shard_map/ppermute | solution.py:32
  30.3 2.3 copy-start.3
  30.3 4.9 %copy-start.7 = (bf16[2,4,90,256]{3,1,2,0:T(4,128)(2,1)S(1)}, bf16[2,4,90,256]{3,1,2,0:T(4,128)(2,1)}, u32[]{:S(2)}) copy-start(bf16[2,4,90,256]{3,1,2,0:T(4,128)(2,1)} %param.6) | copy-start | bytes 1105924
  32.7 2.7 copy-start.6
  32.7 21.9 %copy-start.9 = (f32[2,256]{1,0:T(2,128)S(1)}, f32[2,256]{1,0:T(2,128)}, u32[]{:S(2)}) copy-start(f32[2,256]{1,0:T(2,128)} %param.11) | copy-start | bytes 6148
  35.2 118.8 %reduce-scatter.6.cloned.1.call-start = ((), (), s32[]{:S(2)}) async-start(), calls=%async_computation.4 | async-start | bytes 1179648 | tf_op jit(solution)/shard_map/reduce_scatter | solution.py:104
  75.9 4.6 %collective-permute-start.3 = (bf16[2,1,90,128]{3,2,1,0:T(8,128)(2,1)S(1)}, bf16[2,1,90,128]{3,2,1,0:T(8,128)(2,1)S(1)}, u32[]{:S(2)}, u32[]{:S(2)}) collective-permute-start(bf16[2,1,90,128]{3,2,1,0:T(8,128)(2,1)S(1)} %get-tuple-element.38), channel_id=1, source_target_pairs={{0,2},{1,3},{4,6},{5,7},{8,10},{9,11},{12,14},{13,15},{16,18},{17,... | collective-permute-start | bytes 138248 | tf_op jit(solution)/shard_map/ppermute | solution.py:20
  78.8 6.0 %collective-permute-start.4 = (bf16[2,1,90,128]{3,2,1,0:T(8,128)(2,1)S(1)}, bf16[2,1,90,128]{3,2,1,0:T(8,128)(2,1)S(1)}, u32[]{:S(2)}, u32[]{:S(2)}) collective-permute-start(bf16[2,1,90,128]{3,2,1,0:T(8,128)(2,1)S(1)} %get-tuple-element.39), channel_id=1, source_target_pairs={{2,0},{3,1},{6,4},{7,5},{10,8},{11,9},{14,12},{15,13},{18,16},{19,... | collective-permute-start | bytes 138248 | tf_op jit(solution)/shard_map/ppermute | solution.py:22
  84.8 8.6 %collective-permute-start.5 = (bf16[2,6,90,128]{3,2,1,0:T(8,128)(2,1)S(1)}, bf16[2,6,90,128]{3,2,1,0:T(8,128)(2,1)S(1)}, u32[]{:S(2)}, u32[]{:S(2)}) collective-permute-start(bf16[2,6,90,128]{3,2,1,0:T(8,128)(2,1)S(1)} %pad_maximum_fusion.3), channel_id=1, source_target_pairs={{4,0},{8,4},{12,8},{5,1},{9,5},{13,9},{6,2},{10,6},{14,10},{7,3},{... | collective-permute-start | bytes 829448 | tf_op jit(solution)/shard_map/ppermute | solution.py:32
  94.2 1.5 copy-start.10
  95.2 2.3 copy-start.4
  95.6 3.1 %copy-start.8 = (bf16[2,4,90,256]{3,1,2,0:T(4,128)(2,1)S(1)}, bf16[2,4,90,256]{3,1,2,0:T(4,128)(2,1)}, u32[]{:S(2)}) copy-start(bf16[2,4,90,256]{3,1,2,0:T(4,128)(2,1)} %param.6) | copy-start | bytes 1105924
  97.5 1.6 copy-start.5
  98.5 182.5 %reduce-scatter.8.cloned.1.call-start = ((), (), s32[]{:S(2)}) async-start(), calls=%async_computation.5 | async-start | bytes 7962624 | tf_op jit(solution)/shard_map/reduce_scatter | solution.py:152
  146.2 4.3 %copy-start.2 = (f32[256,1,3,3,3,128]{5,0,4,3,2,1:T(8,128)S(1)}, f32[256,1,3,3,3,128]{5,0,4,3,2,1:T(8,128)}, u32[]{:S(2)}) copy-start(f32[256,1,3,3,3,128]{5,0,4,3,2,1:T(8,128)} %convolution_bitcast_fusion) | copy-start | bytes 10616836
  153.9 129.2 %copy-start.1 = (bf16[256,3,3,3,128]{4,0,3,2,1:T(8,128)(2,1)S(1)}, bf16[256,3,3,3,128]{4,0,3,2,1:T(8,128)(2,1)}, u32[]{:S(2)}) copy-start(bf16[256,3,3,3,128]{4,0,3,2,1:T(8,128)(2,1)} %param.10) | copy-start | bytes 5308420
Sparse Core Ops, SparseCore 0:
  35.3 7.4 reduce-scatter.3
  98.6 5.4 reduce-scatter.5
  154.0 126.9 reduce-scatter.7
where the time goes:
time: 291 us; the launch traced here: 290 us
  waiting for transfers between devices  127 us (44%)
  blocking collectives  54.5 us (19%)
  local copies, waits for them, and re-layouts  54.4 us (19%)
  matrix products  14.5 us (5%)
  between operations  14.3 us (5%)
  starting transfers between devices  13.2 us (5%)
  other arithmetic  11.5 us (4%)
    reduce_scatter x1, waiting for transfers between devices, shards(): lax.psum_scatter(jnp.stack([term_one(start, lax.axis_size(('tm', 'space')...  104 us
    psum x3, blocking collectives, clip_totals(): return lax.psum(values, ('tm', 'space'))  54.5 us
    unnamed x73, local copies, waits for them, and re-layouts  21.3 us
    dot_general x2, local copies, waits for them, and re-layouts, term(): lax.dot_general(flat_active, flat_taps, (((0,), (0,)), ((), ())), preferr...  15.9 us
    ppermute x2, waiting for transfers between devices, passed_along(): return lax.ppermute(block, axis, route)  14.5 us
    another operation x4, local copies, waits for them, and re-layouts, tap_stack(): stacked = jnp.stack(pieces, axis=3)  10.6 us
    dot_general x2, matrix products, term(): lax.dot_general(flat_active, flat_taps, (((0,), (0,)), ((), ())), preferr...  10.3 us
    ppermute x2, waiting for transfers between devices, extended_2(): lax.ppermute(head, axis, [((i + 1) % count, i) for i in range(ends)])  8.45 us
  transfers between devices with their start and end apart: 9, of which 7 were waited for; matrix products, arithmetic and copies ran while one was open for 22% of the time, Pallas kernels for 0%

commit v1 on v0

v1 whole, which is shorter than its diff:
```python
import functools

import jax
import jax.numpy as jnp
from jax import lax
from jax.experimental import pallas as pl
from jax.experimental.pallas import tpu as pltpu
from jax.sharding import PartitionSpec as P

GROUPS = 32
EPS = 1e-06
MESH = pl.DeviceIdType.MESH
F32 = jnp.float32
BF16 = jnp.bfloat16


def group_sums(values, per):
    channels = values.shape[1]
    row = lax.broadcasted_iota(jnp.int32, (channels, channels), 0) // per
    col = lax.broadcasted_iota(jnp.int32, (channels, channels), 1) // per
    same = jnp.where(row == col, 1.0, 0.0).astype(F32)
    return jnp.dot(values, same, precision=lax.Precision.HIGHEST, preferred_element_type=F32)


def body(
    sizes,
    f_ref, h_ref, cot_ref, k1_ref, k2_ref, gain_ref,
    fg_ref, d1_ref, d2_ref, w_ref,
    ext2, ext1, gh, taps, act1, act2, acc,
    xs2, xr2, xs1, xr1, vec, r0, r2, r1, dd2, dd1, rr2, rr1,
    halo_s, halo_r, xsem_s, xsem_r, ar_s, ar_r, dl_s, dl_r,
):
    width, n_t, n_s = sizes
    frames, height, padded, half = cot_ref.shape
    channels = f_ref.shape[3]
    per = channels // GROUPS
    n = n_t * n_s
    rows = frames * height * padded
    block = height * padded
    share = channels // n
    t = lax.axis_index("tm")
    s = lax.axis_index("space")
    chan = lax.axis_index("chan")
    partner = 1 - chan
    rank = t * n_s + s
    members = float(frames * height * width * per * n)
    mine = pl.ds(pl.multiple_of(chan * half, half), half)
    theirs = pl.ds(pl.multiple_of(partner * half, half), half)

    def place(j):
        return {"tm": j // n_s, "space": lax.rem(j, n_s)}

    def peer(k):
        return lax.rem(rank + k, n)

    def each_peer(fn):
        def step(k, carry):
            fn(k)
            return carry

        lax.fori_loop(1, n, step, 0)

    ext2[...] = jnp.zeros_like(ext2)
    ext1[...] = jnp.zeros_like(ext1)

    barrier = pltpu.get_barrier_semaphore()
    pl.semaphore_signal(barrier, inc=1, device_id={"chan": partner}, device_id_type=MESH)
    each_peer(
        lambda k: pl.semaphore_signal(barrier, inc=1, device_id=place(peer(k)), device_id_type=MESH)
    )
    pl.semaphore_wait(barrier, n)

    last = height - 1
    below = (slice(0, frames), slice(height + 1, height + 2))
    above = (slice(0, frames), slice(0, 1))
    later = slice(frames, frames + 2)
    moves = (
        (0, -1, (slice(0, frames), slice(0, 1)), below),
        (0, 1, (slice(0, frames), slice(last, last + 1)), above),
        (-1, 0, (slice(0, 2), slice(0, height)), (later, slice(1, height + 1))),
        (-1, -1, (slice(0, 2), slice(0, 1)), (later, slice(height + 1, height + 2))),
        (-1, 1, (slice(0, 2), slice(last, last + 1)), (later, slice(0, 1))),
    )

    def inside(dt, ds):
        ok = None
        for value, step, count in ((t, dt, n_t), (s, ds, n_s)):
            if step:
                now = (value + step >= 0) & (value + step < count)
                ok = now if ok is None else ok & now
        return ok

    def halo(layer, source, dest, m):
        dt, ds, src, dst = moves[m]
        return pltpu.make_async_remote_copy(
            src_ref=source.at[src], dst_ref=dest.at[dst],
            send_sem=halo_s.at[layer, m], recv_sem=halo_r.at[layer, m],
            device_id={"tm": t + dt, "space": s + ds}, device_id_type=MESH,
        )

    def halo_start(layer, source, dest):
        for m in (2, 0, 1, 3, 4):
            @pl.when(inside(moves[m][0], moves[m][1]))
            def _(m=m):
                halo(layer, source, dest, m).start()

    def halo_arrive(layer, source, dest):
        for m in (2, 0, 1, 3, 4):
            @pl.when(inside(-moves[m][0], -moves[m][1]))
            def _(m=m):
                halo(layer, source, dest, m).wait_recv()

    def halo_end(layer, source, dest):
        for m in (2, 0, 1, 3, 4):
            @pl.when(inside(moves[m][0], moves[m][1]))
            def _(m=m):
                halo(layer, source, dest, m).wait_send()

    def sums_copy(layer, buf, k, slot):
        return pltpu.make_async_remote_copy(
            src_ref=buf.at[slot], dst_ref=buf.at[slot],
            send_sem=ar_s.at[layer, k], recv_sem=ar_r.at[layer, slot],
            device_id=place(peer(k)), device_id_type=MESH,
        )

    def sums_start(layer, buf, values):
        buf[rank] = values
        each_peer(lambda k: sums_copy(layer, buf, k, rank).start())

    def sums_finish(layer, buf):
        each_peer(lambda k: sums_copy(layer, buf, k, peer(k)).wait_recv())
        return jnp.sum(buf[...], axis=0)

    def sums_end(layer, buf):
        each_peer(lambda k: sums_copy(layer, buf, k, rank).wait_send())

    def share_copy(layer, out, buf, k, target, slot):
        return pltpu.make_async_remote_copy(
            src_ref=out.at[target], dst_ref=buf.at[slot],
            send_sem=dl_s.at[layer, k], recv_sem=dl_r.at[layer, slot],
            device_id=place(peer(k)), device_id_type=MESH,
        )

    def cross(layer, source, dest, f):
        return pltpu.make_async_remote_copy(
            src_ref=source.at[f], dst_ref=dest.at[f],
            send_sem=xsem_s.at[layer, f], recv_sem=xsem_r.at[layer, f],
            device_id={"chan": partner}, device_id_type=MESH,
        )

    column = lax.rem(lax.broadcasted_iota(jnp.int32, (rows, 1), 0), padded)
    real = column < width

    halo_start(0, cot_ref, ext2)
    ext2[0:frames, 1 : height + 1] = cot_ref[...]
    field_one = f_ref[...].reshape(rows, channels).astype(F32)
    field_two = h_ref[...].reshape(rows, channels).astype(F32)
    parts = [
        jnp.sum(field_one, axis=0, keepdims=True),
        jnp.sum(field_one * field_one, axis=0, keepdims=True),
        jnp.sum(field_two, axis=0, keepdims=True),
        jnp.sum(field_two * field_two, axis=0, keepdims=True),
        jnp.zeros((4, channels), F32),
    ]
    sums_start(0, r0, jnp.concatenate(parts, axis=0))

    def fill_taps(ext):
        def step(f, carry):
            cells = ext[f].reshape((height + 2) * padded, half).astype(F32)
            size = cells.shape[0]
            ahead = pltpu.roll(cells, size - 1, 0)
            behind = pltpu.roll(cells, 1, 0)
            for c, value in enumerate((ahead, cells, behind)):
                taps[f, :, :, c * half : (c + 1) * half] = value.astype(BF16).reshape(
                    height + 2, padded, half
                )
            return carry

        lax.fori_loop(0, frames + 2, step, 0)

    def conv(kernel, layer, source, dest):
        def step(f, carry):
            total = None
            for ab in range(9):
                a, b = ab // 3, ab % 3
                left = taps[2 - a + f, 2 - b : 2 - b + height].reshape(block, 3 * half)
                term = lax.dot_general(
                    left, kernel[ab], (((1,), (1,)), ((), ())), preferred_element_type=F32
                )
                total = term if total is None else total + term
            acc[f] = total
            source[f] = acc[f, :, theirs].astype(BF16)
            cross(layer, source, dest, f).start()
            return carry

        lax.fori_loop(0, frames, step, 0)

    def delta(act, out, own):
        def step(ab, carry):
            a = ab // 3
            b = lax.rem(ab, 3)
            right = taps[pl.ds(2 - a, frames), pl.ds(2 - b, height)].reshape(rows, 3 * half)
            product = jnp.dot(act[...], right, preferred_element_type=F32)
            small = product.astype(BF16)
            for j in range(n):
                out[j, ab] = small[j * share : (j + 1) * share]

                @pl.when(rank == j)
                def _(j=j):
                    own[ab] = product[j * share : (j + 1) * share]

            return carry

        lax.fori_loop(0, 9, step, 0)

    halo_arrive(0, cot_ref, ext2)
    fill_taps(ext2)
    conv(k2_ref, 0, xs2, xr2)

    totals = group_sums(sums_finish(0, r0), per) / members
    mean_one, mean_two = totals[0:1], totals[2:3]
    scale_one = lax.rsqrt(totals[1:2] - mean_one * mean_one + EPS)
    scale_two = lax.rsqrt(totals[3:4] - mean_two * mean_two + EPS)
    vec[0:1] = mean_one
    vec[1:2] = scale_one
    vec[2:3] = gain_ref[0:1]
    vec[3:4] = mean_two
    vec[4:5] = scale_two
    vec[5:6] = gain_ref[1:2]

    def activate(field_ref, base, act):
        field = field_ref[...].reshape(rows, channels).astype(F32)
        scaled = (field - vec[base : base + 1]) * vec[base + 1 : base + 2] * vec[base + 2 : base + 3]
        active = jnp.where(real, scaled * jax.nn.sigmoid(scaled), 0.0)
        act[...] = active.T.astype(BF16)

    activate(h_ref, 3, act2)
    delta(act2, dd2, d2_ref)

    def norm_back(field_ref, base, layer, dest, buf, w_row):
        for f in range(frames):
            cross(layer, xs2 if layer == 0 else xs1, dest, f).wait_recv()
        upstream = acc[:, :, mine].reshape(rows, half) + dest[...].reshape(rows, half).astype(F32)
        field = field_ref[:, :, :, mine].reshape(rows, half).astype(F32)
        scale = vec[base + 1 : base + 2, mine]
        gain = vec[base + 2 : base + 3, mine]
        centred = (field - vec[base : base + 1, mine]) * scale
        scaled = centred * gain
        gate = jax.nn.sigmoid(scaled)
        slope = jnp.where(real, upstream * gate * (1.0 + scaled * (1.0 - gate)), 0.0)
        parts = [
            jnp.sum(slope, axis=0, keepdims=True),
            jnp.sum(slope * centred, axis=0, keepdims=True),
            jnp.zeros((6, half), F32),
        ]
        sums_start(layer + 1, buf, jnp.concatenate(parts, axis=0))
        totals = sums_finish(layer + 1, buf)
        w_ref[w_row : w_row + 1] = totals[1:2]
        means = group_sums(totals * gain, per) / members
        grad = scale * (slope * gain - means[0:1] - centred * means[1:2])
        return jnp.where(real, grad, 0.0)

    grad_hidden = norm_back(h_ref, 3, 0, xr2, r2, 1).astype(BF16)
    gh[...] = grad_hidden.reshape(frames, height, padded, half)
    halo_start(1, gh, ext1)
    each_peer(lambda k: share_copy(0, dd2, rr2, k, peer(k), rank).start())
    ext1[0:frames, 1 : height + 1] = gh[...]
    activate(f_ref, 0, act1)
    halo_arrive(1, gh, ext1)
    fill_taps(ext1)
    conv(k1_ref, 1, xs1, xr1)
    delta(act1, dd1, d1_ref)
    each_peer(lambda k: share_copy(1, dd1, rr1, k, peer(k), rank).start())
    grad = norm_back(f_ref, 0, 1, xr1, r1, 0)
    fg_ref[...] = (cot_ref[...].reshape(rows, half).astype(F32) + grad).astype(BF16)

    def collect(layer, out, buf, own):
        def step(k, carry):
            share_copy(layer, out, buf, k, peer(k), peer(k)).wait_recv()
            own[...] += buf[peer(k)].astype(F32)
            return carry

        lax.fori_loop(1, n, step, 0)

    collect(0, dd2, rr2, d2_ref)
    collect(1, dd1, rr1, d1_ref)

    halo_end(0, cot_ref, ext2)
    halo_end(1, gh, ext1)
    sums_end(0, r0)
    sums_end(1, r2)
    sums_end(2, r1)
    for f in range(frames):
        cross(0, xs2, xr2, f).wait_send()
        cross(1, xs1, xr1, f).wait_send()
    each_peer(lambda k: share_copy(0, dd2, rr2, k, peer(k), rank).wait_send())
    each_peer(lambda k: share_copy(1, dd1, rr1, k, peer(k), rank).wait_send())


def shards(n_t, n_s, features, hidden, cotangent, kernel_one, kernel_two, gains):
    frames, height, width, channels = features.shape
    half = kernel_one.shape[4]
    padded = -(-width // 16) * 16
    if padded < width + 1:
        padded += 16
    n = n_t * n_s
    share = channels // n
    rows = frames * height * padded
    block = height * padded
    offset = lax.axis_index("chan") * half

    def wide(field):
        return jnp.pad(field, ((0, 0), (0, 0), (0, padded - width), (0, 0)))

    def stacked(kernel):
        return kernel.reshape(channels, 9, 3 * half).transpose(1, 0, 2)

    cot = wide(lax.dynamic_slice_in_dim(cotangent, offset, half, 3))
    vmem = pl.BlockSpec(memory_space=pltpu.VMEM)
    ext = pltpu.VMEM((frames + 2, height + 2, padded, half), BF16)
    halves = pltpu.VMEM((frames, block, half), BF16)
    pieces = pltpu.VMEM((n, 9, share, 3 * half), BF16)
    dma = pltpu.SemaphoreType.DMA
    grad, delta_one, delta_two, weighted = pl.pallas_call(
        functools.partial(body, (width, n_t, n_s)),
        out_shape=(
            jax.ShapeDtypeStruct((rows, half), BF16),
            jax.ShapeDtypeStruct((9, share, 3 * half), F32),
            jax.ShapeDtypeStruct((9, share, 3 * half), F32),
            jax.ShapeDtypeStruct((2, half), F32),
        ),
        in_specs=[vmem] * 6,
        out_specs=(vmem,) * 4,
        scratch_shapes=[
            ext,
            ext,
            pltpu.VMEM((frames, height, padded, half), BF16),
            pltpu.VMEM((frames + 2, height + 2, padded, 3 * half), BF16),
            pltpu.VMEM((channels, rows), BF16),
            pltpu.VMEM((channels, rows), BF16),
            pltpu.VMEM((frames, block, channels), F32),
            halves,
            halves,
            halves,
            halves,
            pltpu.VMEM((8, channels), F32),
            pltpu.VMEM((n, 8, channels), F32),
            pltpu.VMEM((n, 8, half), F32),
            pltpu.VMEM((n, 8, half), F32),
            pieces,
            pieces,
            pieces,
            pieces,
            dma((2, 5)),
            dma((2, 5)),
            dma((2, frames)),
            dma((2, frames)),
            dma((3, n)),
            dma((3, n)),
            dma((2, n)),
            dma((2, n)),
        ],
        compiler_params=pltpu.CompilerParams(
            collective_id=0, has_side_effects=True, vmem_limit_bytes=63 * 1024 * 1024
        ),
    )(wide(features), wide(hidden), cot, stacked(kernel_one), stacked(kernel_two), gains)

    def unstacked(delta):
        return delta.transpose(1, 0, 2).reshape(share, 3, 3, 3, half)

    feature_grad = grad.reshape(frames, height, padded, half)[:, :, :width]
    return (feature_grad, unstacked(delta_one), unstacked(delta_two), weighted)


def solution(mesh):
    placed = (
        P(("clip", "tm"), "space", None, None),
        P(("clip", "tm"), "space", None, None),
        P(("clip", "tm"), "space", None, None),
        P(None, None, None, None, "chan"),
        P(None, None, None, None, "chan"),
        P(),
    )
    return jax.shard_map(
        functools.partial(shards, mesh.shape["tm"], mesh.shape["space"]),
        mesh=mesh,
        in_specs=placed,
        out_specs=(
            P(("clip", "tm"), "space", None, "chan"),
            P(("clip", "tm", "space"), None, None, None, "chan"),
            P(("clip", "tm", "space"), None, None, None, "chan"),
            P("clip", "chan"),
        ),
        check_vma=False,
    )
```

time: 291 us -> 130 us (0.45)
  waiting for transfers between devices: 127 us -> 0 us
  Pallas kernels: 0 us -> 112 us
  blocking collectives: 54.5 us -> 0 us
  local copies, waits for them, and re-layouts: 54.4 us -> 17.5 us
  matrix products: 14.5 us -> 0 us
  between operations: 14.3 us -> 0.74 us
  starting transfers between devices: 13.2 us -> 0 us
  other arithmetic: 11.5 us -> 0 us
    pallas_call x0 -> x1, Pallas kernels: none -> 112 us  [shards(): pl.pallas_call(functools.partial(body, (width, n_t, n_s)), out_shape=(jax...]
    reduce_scatter x3 -> x0, waiting for transfers between devices: 104 us -> none  [the longest x1 104 us: shards(): lax.psum_scatter(jnp.stack([term_one(start, lax.axis_size(('tm', 'space')...]
    psum x3 -> x0, blocking collectives: 54.5 us -> none  [clip_totals(): return lax.psum(values, ('tm', 'space'))]
    ppermute x6 -> x0, waiting for transfers between devices: 23.8 us -> none  [the longest x2 14.5 us: passed_along(): return lax.ppermute(block, axis, route)]
    dot_general x3 -> x0, local copies, waits for them, and re-layouts: 16.8 us -> none  [the longest x2 15.9 us: term(): lax.dot_general(flat_active, flat_taps, (((0,), (0,)), ((), ())), preferr...]
    dot_general x4 -> x0, matrix products: 14.5 us -> none  [the longest x2 10.3 us: term(): lax.dot_general(flat_active, flat_taps, (((0,), (0,)), ((), ())), preferr...]
    ppermute x6 -> x0, starting transfers between devices: 12.9 us -> none  [the longest x2 7.73 us: extended_2(): lax.ppermute(tail, axis, [(i, (i + 1) % count) for i in range(ends)])]
    unnamed x73 -> x21, local copies, waits for them, and re-layouts: 21.3 us -> 9.32 us
  transfers between devices with their start and end apart: 9 -> 0, of which waited for: 7 -> 0; matrix products, arithmetic and copies ran while one was open for 22% -> 0% of each run, Pallas kernels for 0% -> 0%
where the time goes in v1:
time: 130 us
  Pallas kernels  112 us (86%)
  local copies, waits for them, and re-layouts  17.5 us (13%)
    pallas_call x1, Pallas kernels, shards(): pl.pallas_call(functools.partial(body, (width, n_t, n_s)), out_shape=(jax...  112 us
    unnamed x21, local copies, waits for them, and re-layouts  9.32 us
    reshape x2, local copies, waits for them, and re-layouts, stacked(): return kernel.reshape(channels, 9, 3 * half).transpose(1, 0, 2)  4.49 us

profile of v1, /device:TPU:0, one launch (start us, length us, event | category | flops | bytes accessed | tf_op | source)
XLA Modules:
  0.0 130.0 jit_solution(15392125585109324736)
XLA Ops:
  0.6 0.0 copy-start
  0.6 1.0 copy-done
  1.6 0.1 constant_dynamic-slice_fusion
  1.7 0.7 pad.13.cot_ref
  2.4 2.6 %copy.21 = bf16[256,3,3,3,128]{0,4,3,2,1:T(8,128)(2,1)S(1)} copy(bf16[256,3,3,3,128]{4,0,3,2,1:T(8,128)(2,1)} %param.9) | data formatting | bytes 3538944 | tf_op args[3]
  5.1 2.3 %copy.22 = bf16[256,9,384]{2,0,1:T(8,128)(2,1)} copy(bf16[256,9,384]{0,2,1:T(8,128)(2,1)S(1)} %bitcast.12) | data formatting | bytes 3538944 | tf_op jit(solution)/shard_map/reshape | solution.py:316
  7.3 2.6 %copy.23 = bf16[256,3,3,3,128]{0,4,3,2,1:T(8,128)(2,1)S(1)} copy(bf16[256,3,3,3,128]{4,0,3,2,1:T(8,128)(2,1)} %param.10) | data formatting | bytes 3538944 | tf_op args[4]
  9.9 0.0 copy-start.2
  10.0 0.0 copy-start.3
  10.0 2.2 %copy.24 = bf16[256,9,384]{2,0,1:T(8,128)(2,1)} copy(bf16[256,9,384]{0,2,1:T(8,128)(2,1)S(1)} %bitcast.13) | data formatting | bytes 3538944 | tf_op jit(solution)/shard_map/reshape | solution.py:316
  12.2 0.0 copy-done.2
  12.2 0.8 pad.11.f_ref
  13.0 0.0 copy-done.3
  13.1 0.8 pad.12.h_ref
  13.9 111.7 %shard_map.93 = (bf16[768,128]{1,0:T(8,128)(2,1)}, f32[9,32,384]{2,1,0:T(8,128)}, f32[9,32,384]{2,1,0:T(8,128)}, f32[2,128]{1,0:T(2,128)}) custom-call(bf16[2,4,96,256]{3,2,1,0:T(8,128)(2,1)} %pad.11.f_ref, bf16[2,4,96,256]{3,2,1,0:T(8,128)(2,1)} %pad.12.h_ref, bf16[2,4,96,128]{3,2,1,0:T(8,128)(2,1)} %pad.13.cot_ref, bf16[9,256,384]{2,1,0:T(8,128)(2,1)} %bitcast.14, ...), custom_call_target="tpu_custom_call" | custom-call | tf_op jit(solution)/shard_map/pallas_call | solution.py:324
  125.6 0.0 copy-start.1
  125.6 1.2 reshape.26
  126.8 0.0 copy-start.4
  126.8 0.8 copy.26
  127.7 0.2 reshape.27
  127.8 0.8 copy.27
  128.6 0.0 copy-done.4
  128.7 0.8 copy.29
  129.4 0.6 copy.31
  (6 shorter events, 0.1 us)
Async XLA Ops:
  0.6 1.0 copy-start
  9.9 2.3 %copy-start.2 = (bf16[2,4,90,256]{3,1,2,0:T(4,128)(2,1)S(1)}, bf16[2,4,90,256]{3,1,2,0:T(4,128)(2,1)}, u32[]{:S(2)}) copy-start(bf16[2,4,90,256]{3,1,2,0:T(4,128)(2,1)} %param.6) | copy-start | bytes 1105924
  10.0 3.1 %copy-start.3 = (bf16[2,4,90,256]{3,1,2,0:T(4,128)(2,1)S(1)}, bf16[2,4,90,256]{3,1,2,0:T(4,128)(2,1)}, u32[]{:S(2)}) copy-start(bf16[2,4,90,256]{3,1,2,0:T(4,128)(2,1)} %param.7) | copy-start | bytes 1105924
  125.6 2.1 %copy-start.1 = (f32[9,32,384]{2,1,0:T(8,128)S(1)}, f32[9,32,384]{2,1,0:T(8,128)}, u32[]{:S(2)}) copy-start(f32[9,32,384]{2,1,0:T(8,128)} %get-tuple-element.10) | copy-start | bytes 1327108
  126.8 1.8 %copy-start.4 = (bf16[768,128]{1,0:T(8,128)(2,1)S(1)}, bf16[768,128]{1,0:T(8,128)(2,1)}, u32[]{:S(2)}) copy-start(bf16[768,128]{1,0:T(8,128)(2,1)} %get-tuple-element.8) | copy-start | bytes 589828
  126.8 2.6 %copy-start.5 = (f32[2,128]{1,0:T(2,128)S(1)}, f32[2,128]{1,0:T(2,128)}, u32[]{:S(2)}) copy-start(f32[2,128]{1,0:T(2,128)} %get-tuple-element.27) | copy-start | bytes 3076
